TPU v7x, 32 devices: a whole 2x2x4 slice. The times are simulated.
32 devices in a mesh: gx: 8 (over z, y), gy: 4 (over x, core).
Axes of the slice: x: 2, y: 2, z: 4, core: 2. Of those that a mesh axis runs over, the one named last changes fastest.
Arguments:
- modes: float32 [16, 3, 32, 32, 128], P(None, None, 'gx', 'gy'), may hold values from -0.03 to 0.03
- region: int32 [32, 32, 128], P('gx', 'gy'), may hold values from 0 to 15
- stiffness: float32 [16], replicated, may hold values from 0.1 to 10
- coarse_group: int32 [8, 4], replicated, may hold values from 0 to 3
Outputs:
- coarse: float32 [8, 64, 192], P('gx', 'gy')
All inputs are finite; a program needn't handle non-finite values.
Results may differ from a plain program's by a relative error of at most 0.0003.
Values sent between devices are 32-bit elements; how exact they have to be, the bound alone decides.
A program may use at most 128 MiB of HBM per device.

v0:
```python
import jax
import jax.numpy as jnp
from jax import lax
from jax.sharding import PartitionSpec as P

GROUPS = 4


beta_shear = 0.5
mass_share = 0.1


def extended(cells, sides, width):
    for axis, dim in sides:
        count = lax.axis_size(axis)
        ends = count - 1
        head = lax.slice_in_dim(cells, 0, width, axis=dim)
        tail = lax.slice_in_dim(cells, cells.shape[dim] - width, cells.shape[dim], axis=dim)
        cells = jnp.concatenate(
            [
                lax.ppermute(tail, axis, [(i, (i + 1) % count) for i in range(ends)]),
                cells,
                lax.ppermute(head, axis, [((i + 1) % count, i) for i in range(ends)]),
            ],
            axis=dim,
        )
    return cells


def all_offsets():
    return [
        (shift_x, shift_y, shift_z)
        for shift_x in (-1, 0, 1)
        for shift_y in (-1, 0, 1)
        for shift_z in (-1, 0, 1)
        if (shift_x, shift_y, shift_z) != (0, 0, 0)
    ]


def apply_operator(padded, stiff_pad):
    span_x = padded.shape[2] - 2
    span_y = padded.shape[3] - 2
    span_z = padded.shape[4] - 2
    centre = padded[:, :, 1 : span_x + 1, 1 : span_y + 1, 1 : span_z + 1]
    stiff_here = stiff_pad[1 : span_x + 1, 1 : span_y + 1, 1 : span_z + 1]
    result = mass_share * stiff_here * centre
    for step_x, step_y, step_z in all_offsets():
        reach_len = abs(step_x) + abs(step_y) + abs(step_z)
        weight = 0.5 ** (reach_len - 1)
        nearby = padded[
            :,
            :,
            1 + step_x : 1 + step_x + span_x,
            1 + step_y : 1 + step_y + span_y,
            1 + step_z : 1 + step_z + span_z,
        ]
        stiff_there = stiff_pad[
            1 + step_x : 1 + step_x + span_x,
            1 + step_y : 1 + step_y + span_y,
            1 + step_z : 1 + step_z + span_z,
        ]
        coupling = 0.5 * weight * (stiff_here + stiff_there)
        differ = centre - nearby
        along_dir = (
            beta_shear
            / reach_len
            * (step_x * differ[:, 0] + step_y * differ[:, 1] + step_z * differ[:, 2])
        )
        pushed = differ + jnp.stack(
            [step_x * along_dir, step_y * along_dir, step_z * along_dir], axis=1
        )
        result = result + coupling * pushed
    return result


def contract(left_side, right_side):
    return jnp.einsum("kaxyz,jaxyz->kj", left_side, right_side, precision=lax.Precision.HIGHEST)


def pair_blocks(applied, mode_cycle):
    span_x = mode_cycle.shape[2] - 2
    span_y = mode_cycle.shape[3] - 2
    bounds_x = [(0, 1), (1, span_x + 1), (span_x + 1, span_x + 2)]
    bounds_y = [(0, 1), (1, span_y + 1), (span_y + 1, span_y + 2)]
    rows_out = []
    for low_x, high_x in bounds_x:
        cols_out = []
        for low_y, high_y in bounds_y:
            cols_out.append(
                contract(
                    applied[:, :, low_x:high_x, low_y:high_y],
                    mode_cycle[:, :, low_x:high_x, low_y:high_y],
                )
            )
        rows_out.append(jnp.stack(cols_out))
    return jnp.stack(rows_out)


def shards(modes, region, stiffness, coarse_group):
    width = modes.shape[0]
    levels = jnp.arange(stiffness.shape[0], dtype=jnp.int32)
    stiff_cells = jnp.sum(jnp.where(region[..., None] == levels, stiffness, 0.0), axis=-1)
    stiff_cycle = extended(stiff_cells, (("gx", 0), ("gy", 1)), 1)
    stiff_pad = jnp.pad(stiff_cycle, ((1, 1), (1, 1), (1, 1)))
    padded = jnp.pad(modes, ((0, 0), (0, 0), (2, 2), (2, 2), (1, 1)))
    applied = apply_operator(padded, stiff_pad)
    group_pad = jnp.pad(coarse_group, 1, constant_values=-1)
    neighbours = lax.dynamic_slice(group_pad, (lax.axis_index("gx"), lax.axis_index("gy")), (3, 3))
    labels = jnp.arange(GROUPS, dtype=jnp.int32)
    hot_near = (neighbours[..., None] == labels).astype(jnp.float32)
    hot_self = hot_near[1, 1]
    mode_cycle = extended(modes, (("gx", 2), ("gy", 3)), 1)
    pair_nine = pair_blocks(applied, mode_cycle)
    partial_value = jnp.einsum(
        "g,xykj,xyh->gkxhj", hot_self, pair_nine, hot_near, precision=lax.Precision.HIGHEST
    )
    partial_value = partial_value.reshape(GROUPS * width, 3 * GROUPS * width)
    coarse_rows = lax.psum_scatter(partial_value, "gy", scatter_dimension=0, tiled=True)
    return coarse_rows[None]


def solution(mesh):
    in_specs = (P(None, None, "gx", "gy", None), P("gx", "gy", None), P(), P())
    out_specs = P("gx", "gy", None)
    return jax.shard_map(shards, mesh=mesh, in_specs=in_specs, out_specs=out_specs, check_vma=False)
```

profile of v0, /device:TPU:0, one launch (start us, length us, event | category | flops | bytes accessed | tf_op | source)
XLA Modules:
  0.0 136.5 jit_solution(14644856175629350998)
XLA Ops:
  6.5 0.9 select_reduce_fusion
  7.4 4.9 %collective-permute-start = (f32[1,8,128]{2,1,0:T(8,128)S(1)}, f32[1,8,128]{2,1,0:T(8,128)S(1)}, u32[]{:S(2)}, u32[]{:S(2)}) collective-permute-start(f32[1,8,128]{2,1,0:T(8,128)S(1)} %get-tuple-element.129), channel_id=1, source_target_pairs={{0,4},{4,8},{8,12},{12,16},{16,20},{20,24},{24,28},{1,5},{5,9},{9,... | collective-permute-start | bytes 12296 | tf_op jit(solution)/shard_map/ppermute | solution.py:21
  12.3 1.3 collective-permute-start.1
  13.6 1.6 %copy.24 = f32[16,3,4,8,128]{4,0,1,3,2:T(8,128)S(1)} copy(f32[16,3,4,8,128]{4,3,2,1,0:T(8,128)} %param.4) | data formatting | bytes 1572864 | tf_op args[0]
  15.2 0.8 fusion.182
  16.0 4.5 %collective-permute-start.4 = (f32[16,3,1,8,128]{4,0,1,3,2:T(8,128)}, f32[16,3,1,8,128]{4,0,1,3,2:T(8,128)S(1)}, u32[]{:S(2)}, u32[]{:S(2)}) collective-permute-start(f32[16,3,1,8,128]{4,0,1,3,2:T(8,128)} %get-tuple-element.86), channel_id=1, source_target_pairs={{0,4},{4,8},{8,12},{12,16},{16,20},{20,24},{24,28},{1,5},{5,9},{9,... | collective-permute-start | bytes 589832 | tf_op jit(solution)/shard_map/ppermute | solution.py:21
  20.6 1.3 collective-permute-start.5
  21.9 10.0 %fusion = (f32[16,3,6,10,128]{4,0,1,3,2:T(8,128)}, f32[16,3,6,10,128]{4,0,1,3,2:T(8,128)}, f32[16,3,6,10,128]{4,0,1,3,2:T(8,128)}, f32[16,3,6,10,128]{4,0,1,3,2:...) fusion(f32[16,3,4,8,128]{4,0,1,3,2:T(8,128)S(1)} %copy.24), kind=kLoop, calls=%fused_computation.27 | loop fusion | flops 7004160 | bytes 28803072 | tf_op jit(solution)/shard_map/sub | solution.py:63
  31.9 3.3 %fusion.25 = (f32[16,3,6,10,128]{4,0,1,3,2:T(8,128)}, f32[16,3,6,10,128]{4,0,1,3,2:T(8,128)S(1)}, f32[16,3,6,10,128]{4,0,1,3,2:T(8,128)S(1)}, f32[16,3,6,10,128]...) fusion(f32[16,3,4,8,128]{4,0,1,3,2:T(8,128)S(1)} %copy.24), kind=kLoop, calls=%fused_computation.52 | loop fusion | flops 2580480 | bytes 11108352 | tf_op jit(solution)/shard_map/sub | solution.py:63
  35.4 1.1 broadcast_multiply_fusion.44
  36.5 1.0 broadcast_multiply_fusion.10
  37.6 1.2 broadcast_multiply_fusion.37
  38.8 1.0 broadcast_multiply_fusion.24
  39.9 0.8 copy-done.12
  40.6 1.2 broadcast_multiply_fusion.35
  41.9 1.1 broadcast_multiply_fusion.8
  43.0 1.2 broadcast_multiply_fusion.1
  44.2 1.1 broadcast_multiply_fusion.22
  45.3 1.2 broadcast_multiply_fusion.5
  46.5 1.1 broadcast_multiply_fusion.31
  47.8 3.4 %broadcast_multiply_fusion.13 = (f32[16,1,6,10,128]{4,0,1,3,2:T(8,128)}, f32[16,1,6,10,128]{4,0,1,3,2:T(8,128)}, f32[16,1,6,10,128]{4,0,1,3,2:T(8,128)}, f32[16,1,6,10,128]{4,0,1,3,2:T(8,128)}) fusion(f32[16,3,6,10,128]{4,0,1,3,2:T(8,128)} %get-tuple-element.69, f32[16,3,6,10,128]{4,0,1,3,2:T(8,128)} %get-tuple-element.63), kind=kLoop, calls=%fused_computation.279 | loop fusion | flops 1720320 | bytes 4915200 | tf_op jit(solution)/shard_map/mul | solution.py:70
  51.2 1.4 %broadcast_multiply_fusion.18 = (f32[16,1,6,10,128]{4,0,1,3,2:T(8,128)}, f32[16,1,6,10,128]{4,0,1,3,2:T(8,128)}, f32[16,1,6,10,128]{4,0,1,3,2:T(8,128)}, f32[16,1,6,10,128]{4,0,1,3,2:T(8,128)}) fusion(f32[16,3,6,10,128]{4,0,1,3,2:T(8,128)S(1)} %copy-done.11, f32[16,3,6,10,128]{4,0,1,3,2:T(8,128)S(1)} %copy-done.10), kind=kLoop, calls=%fused_computation.284 | loop fusion | flops 1228800 | bytes 4915200 | tf_op jit(solution)/shard_map/mul | solution.py:70
  52.6 0.7 copy-done.8
  53.7 1.4 %broadcast_multiply_fusion.42 = (f32[16,1,6,10,128]{4,0,1,3,2:T(8,128)}, f32[16,1,6,10,128]{4,0,1,3,2:T(8,128)}, f32[16,1,6,10,128]{4,0,1,3,2:T(8,128)}, f32[16,1,6,10,128]{4,0,1,3,2:T(8,128)}) fusion(f32[16,3,6,10,128]{4,0,1,3,2:T(8,128)S(1)} %copy-done.9, f32[16,3,6,10,128]{4,0,1,3,2:T(8,128)S(1)} %copy-done.8), kind=kLoop, calls=%fused_computation.308 | loop fusion | flops 1720320 | bytes 4915200 | tf_op jit(solution)/shard_map/mul | solution.py:70
  55.1 0.7 copy-done.6
  56.2 1.4 %broadcast_multiply_fusion.29 = (f32[16,1,6,10,128]{4,0,1,3,2:T(8,128)}, f32[16,1,6,10,128]{4,0,1,3,2:T(8,128)}, f32[16,1,6,10,128]{4,0,1,3,2:T(8,128)}, f32[16,1,6,10,128]{4,0,1,3,2:T(8,128)}) fusion(f32[16,3,6,10,128]{4,0,1,3,2:T(8,128)S(1)} %copy-done.6, f32[16,3,6,10,128]{4,0,1,3,2:T(8,128)S(1)} %copy-done.7), kind=kLoop, calls=%fused_computation.295 | loop fusion | flops 1351680 | bytes 4915200 | tf_op jit(solution)/shard_map/mul | solution.py:70
  57.6 0.7 copy-done.4
  58.8 1.4 %broadcast_multiply_fusion.50 = (f32[16,1,6,10,128]{4,0,1,3,2:T(8,128)}, f32[16,1,6,10,128]{4,0,1,3,2:T(8,128)}, f32[16,1,6,10,128]{4,0,1,3,2:T(8,128)}, f32[16,1,6,10,128]{4,0,1,3,2:T(8,128)}) fusion(f32[16,3,6,10,128]{4,0,1,3,2:T(8,128)S(1)} %copy-done.5, f32[16,3,6,10,128]{4,0,1,3,2:T(8,128)S(1)} %copy-done.4), kind=kLoop, calls=%fused_computation.316 | loop fusion | flops 1474560 | bytes 4915200 | tf_op jit(solution)/shard_map/mul | solution.py:65
  60.2 0.7 copy-done.18
  61.3 1.2 fusion.78
  63.5 1.4 %broadcast_multiply_fusion.30 = (f32[16,1,6,10,128]{4,0,1,3,2:T(8,128)}, f32[16,1,6,10,128]{4,0,1,3,2:T(8,128)}, f32[16,1,6,10,128]{4,0,1,3,2:T(8,128)}, f32[16,1,6,10,128]{4,0,1,3,2:T(8,128)}) fusion(f32[16,3,6,10,128]{4,0,1,3,2:T(8,128)S(1)} %copy-done.2, f32[16,3,6,10,128]{4,0,1,3,2:T(8,128)S(1)} %copy-done.3), kind=kLoop, calls=%fused_computation.296 | loop fusion | flops 1228800 | bytes 4915200 | tf_op jit(solution)/shard_map/mul | solution.py:70
  64.9 0.6 copy-done.1
  65.6 1.4 %broadcast_multiply_fusion = (f32[16,1,6,10,128]{4,0,1,3,2:T(8,128)}, f32[16,1,6,10,128]{4,0,1,3,2:T(8,128)}, f32[16,1,6,10,128]{4,0,1,3,2:T(8,128)}, f32[16,1,6,10,128]{4,0,1,3,2:T(8,128)}) fusion(f32[16,3,6,10,128]{4,0,1,3,2:T(8,128)S(1)} %get-tuple-element.81, f32[16,3,6,10,128]{4,0,1,3,2:T(8,128)S(1)} %copy-done.1), kind=kLoop, calls=%fused_computation.266 | loop fusion | flops 1351680 | bytes 4915200 | tf_op jit(solution)/shard_map/mul | solution.py:65
  67.1 1.6 %collective-permute-start.2 = (f32[6,1,128]{2,1,0:T(1,128)S(1)}, f32[6,1,128]{2,1,0:T(1,128)S(1)}, u32[]{:S(2)}, u32[]{:S(2)}) collective-permute-start(f32[6,1,128]{2,1,0:T(1,128)S(1)} %get-tuple-element.127), channel_id=1, source_target_pairs={{0,1},{1,2},{2,3},{4,5},{5,6},{6,7},{8,9},{9,10},{10,11},{12,13},{... | collective-permute-start | bytes 9224 | tf_op jit(solution)/shard_map/ppermute | solution.py:21
  68.6 1.3 collective-permute-start.3
  69.9 3.5 %collective-permute-done.3 = f32[6,1,128]{2,1,0:T(1,128)S(1)} collective-permute-done((f32[6,1,128]{2,1,0:T(1,128)S(1)}, f32[6,1,128]{2,1,0:T(1,128)S(1)}, u32[]{:S(2)}, u32[]{:S(2)}) %collective-permute-start.3) | collective-permute-done | bytes 3104 | tf_op jit(solution)/shard_map/ppermute | solution.py:23
  73.4 0.6 broadcast_multiply_fusion.54
  74.0 1.0 fusion.124
  75.0 0.8 fusion.126
  76.1 14.9 %fusion.74 = f32[16,3,6,10,128]{4,0,1,3,2:T(8,128)S(1)} fusion(f32[16,1,6,10,128]{4,0,1,3,2:T(8,128)} %get-tuple-element.131, f32[16,1,6,10,128]{4,0,1,3,2:T(8,128)} %get-tuple-element.132, f32[16,1,6,10,128]{4,0,1,3,2:T(8,128)} %get-tuple-element.135, f32[16,1,6,10,128]{4,0,1,3,2:T(8,128)} %get-tuple-element.136, ...), kind=kLoop, calls=%fused_computation.125 | loop fusion | flops 56401920 | bytes 30615552 | tf_op jit(solution)/shard_map/add | solution.py:72
  91.0 1.1 copy-done
  92.1 1.4 %convolution_bitcast_fusion = f32[1,16,16]{2,1,0:T(8,128)S(1)} fusion(f32[16,3,4,8,128]{4,3,2,1,0:T(8,128)S(1)} %copy-done, f32[16,3,6,10,128]{4,0,1,3,2:T(8,128)S(1)} %fusion.74), kind=kOutput, calls=%fused_computation.126 | convolution fusion | flops 37748736 | bytes 1573888 | tf_op jit(solution)/shard_map/kaxyz,jaxyz->kj/dot_general | solution.py:77
  94.0 0.9 constant_dynamic-update-slice_fusion
  95.0 4.3 %collective-permute-start.6 = (f32[16,3,6,1,128]{4,0,1,3,2:T(8,128)S(1)}, f32[16,3,6,1,128]{4,0,1,3,2:T(8,128)S(1)}, u32[]{:S(2)}, u32[]{:S(2)}) collective-permute-start(f32[16,3,6,1,128]{4,0,1,3,2:T(8,128)S(1)} %get-tuple-element.57), channel_id=1, source_target_pairs={{0,1},{1,2},{2,3},{4,5},{5,6},{6,7},{8,9},{9,10},{10,11},{12,13},{... | collective-permute-start | bytes 442376 | tf_op jit(solution)/shard_map/ppermute | solution.py:21
  99.2 1.3 collective-permute-start.7
  100.9 1.3 convolution_bitcast_fusion.7
  103.9 0.8 reshape.124
  104.8 24.9 %reduce-scatter.2.cloned.1.call-done = f32[16,192]{1,0:T(8,128)} async-done(((f32[64,192]{1,0:T(8,128)}), f32[16,192]{1,0:T(8,128)}) %reduce-scatter.2.cloned.1.call-update) | async-done | bytes 12304 | tf_op jit(solution)/shard_map/reduce_scatter | solution.py:118
  (113 shorter events, 6.0 us)
Async XLA Ops:
  6.5 123.1 %reduce-scatter.2.cloned.1.call-start = ((), (), s32[]{:S(2)}) async-start(), calls=%async_computation.1 | async-start | bytes 81920 | tf_op jit(solution)/shard_map/reduce_scatter | solution.py:118
  7.4 59.6 %collective-permute-start = (f32[1,8,128]{2,1,0:T(8,128)S(1)}, f32[1,8,128]{2,1,0:T(8,128)S(1)}, u32[]{:S(2)}, u32[]{:S(2)}) collective-permute-start(f32[1,8,128]{2,1,0:T(8,128)S(1)} %get-tuple-element.129), channel_id=1, source_target_pairs={{0,4},{4,8},{8,12},{12,16},{16,20},{20,24},{24,28},{1,5},{5,9},{9,... | collective-permute-start | bytes 12296 | tf_op jit(solution)/shard_map/ppermute | solution.py:21
  12.3 54.7 %collective-permute-start.1 = (f32[1,8,128]{2,1,0:T(8,128)S(1)}, f32[1,8,128]{2,1,0:T(8,128)S(1)}, u32[]{:S(2)}, u32[]{:S(2)}) collective-permute-start(f32[1,8,128]{2,1,0:T(8,128)S(1)} %get-tuple-element.130), channel_id=1, source_target_pairs={{4,0},{8,4},{12,8},{16,12},{20,16},{24,20},{28,24},{5,1},{9,5},{13... | collective-permute-start | bytes 12296 | tf_op jit(solution)/shard_map/ppermute | solution.py:23
  16.0 77.4 %collective-permute-start.4 = (f32[16,3,1,8,128]{4,0,1,3,2:T(8,128)}, f32[16,3,1,8,128]{4,0,1,3,2:T(8,128)S(1)}, u32[]{:S(2)}, u32[]{:S(2)}) collective-permute-start(f32[16,3,1,8,128]{4,0,1,3,2:T(8,128)} %get-tuple-element.86), channel_id=1, source_target_pairs={{0,4},{4,8},{8,12},{12,16},{16,20},{20,24},{24,28},{1,5},{5,9},{9,... | collective-permute-start | bytes 589832 | tf_op jit(solution)/shard_map/ppermute | solution.py:21
  20.6 73.4 %collective-permute-start.5 = (f32[16,3,1,8,128]{4,0,1,3,2:T(8,128)}, f32[16,3,1,8,128]{4,0,1,3,2:T(8,128)}, u32[]{:S(2)}, u32[]{:S(2)}) collective-permute-start(f32[16,3,1,8,128]{4,0,1,3,2:T(8,128)} %get-tuple-element.85), channel_id=1, source_target_pairs={{4,0},{8,4},{12,8},{16,12},{20,16},{24,20},{28,24},{5,1},{9,5},{13... | collective-permute-start | bytes 589832 | tf_op jit(solution)/shard_map/ppermute | solution.py:23
  31.9 3.3 %copy-start.16 = (f32[16,3,6,10,128]{4,0,1,3,2:T(8,128)S(1)}, f32[16,3,6,10,128]{4,0,1,3,2:T(8,128)}, u32[]{:S(2)}) copy-start(f32[16,3,6,10,128]{4,0,1,3,2:T(8,128)} %get-tuple-element.64) | copy-start | bytes 4423684
  31.9 3.3 %copy-start.17 = (f32[16,3,6,10,128]{4,0,1,3,2:T(8,128)S(1)}, f32[16,3,6,10,128]{4,0,1,3,2:T(8,128)}, u32[]{:S(2)}) copy-start(f32[16,3,6,10,128]{4,0,1,3,2:T(8,128)} %get-tuple-element.66) | copy-start | bytes 4423684
  35.4 2.2 %copy-start.14 = (f32[16,3,6,10,128]{4,0,1,3,2:T(8,128)S(1)}, f32[16,3,6,10,128]{4,0,1,3,2:T(8,128)}, u32[]{:S(2)}) copy-start(f32[16,3,6,10,128]{4,0,1,3,2:T(8,128)} %get-tuple-element.70) | copy-start | bytes 4423684
  35.4 2.2 %copy-start.15 = (f32[16,3,6,10,128]{4,0,1,3,2:T(8,128)S(1)}, f32[16,3,6,10,128]{4,0,1,3,2:T(8,128)}, u32[]{:S(2)}) copy-start(f32[16,3,6,10,128]{4,0,1,3,2:T(8,128)} %get-tuple-element.71) | copy-start | bytes 4423684
  37.6 2.3 %copy-start.13 = (f32[16,3,6,10,128]{4,0,1,3,2:T(8,128)S(1)}, f32[16,3,6,10,128]{4,0,1,3,2:T(8,128)}, u32[]{:S(2)}) copy-start(f32[16,3,6,10,128]{4,0,1,3,2:T(8,128)} %get-tuple-element.73) | copy-start | bytes 4423684
  47.8 3.4 %copy-start.10 = (f32[16,3,6,10,128]{4,0,1,3,2:T(8,128)S(1)}, f32[16,3,6,10,128]{4,0,1,3,2:T(8,128)}, u32[]{:S(2)}) copy-start(f32[16,3,6,10,128]{4,0,1,3,2:T(8,128)} %get-tuple-element.61) | copy-start | bytes 4423684
  47.8 3.4 %copy-start.11 = (f32[16,3,6,10,128]{4,0,1,3,2:T(8,128)S(1)}, f32[16,3,6,10,128]{4,0,1,3,2:T(8,128)}, u32[]{:S(2)}) copy-start(f32[16,3,6,10,128]{4,0,1,3,2:T(8,128)} %get-tuple-element.67) | copy-start | bytes 4423684
  51.2 2.1 %copy-start.8 = (f32[16,3,6,10,128]{4,0,1,3,2:T(8,128)S(1)}, f32[16,3,6,10,128]{4,0,1,3,2:T(8,128)}, u32[]{:S(2)}) copy-start(f32[16,3,6,10,128]{4,0,1,3,2:T(8,128)} %get-tuple-element.62) | copy-start | bytes 4423684
  51.2 2.5 %copy-start.9 = (f32[16,3,6,10,128]{4,0,1,3,2:T(8,128)S(1)}, f32[16,3,6,10,128]{4,0,1,3,2:T(8,128)}, u32[]{:S(2)}) copy-start(f32[16,3,6,10,128]{4,0,1,3,2:T(8,128)} %get-tuple-element.68) | copy-start | bytes 4423684
  53.7 2.1 %copy-start.6 = (f32[16,3,6,10,128]{4,0,1,3,2:T(8,128)S(1)}, f32[16,3,6,10,128]{4,0,1,3,2:T(8,128)}, u32[]{:S(2)}) copy-start(f32[16,3,6,10,128]{4,0,1,3,2:T(8,128)} %get-tuple-element.60) | copy-start | bytes 4423684
  53.7 2.5 %copy-start.7 = (f32[16,3,6,10,128]{4,0,1,3,2:T(8,128)S(1)}, f32[16,3,6,10,128]{4,0,1,3,2:T(8,128)}, u32[]{:S(2)}) copy-start(f32[16,3,6,10,128]{4,0,1,3,2:T(8,128)} %get-tuple-element.75) | copy-start | bytes 4423684
  56.2 2.1 %copy-start.4 = (f32[16,3,6,10,128]{4,0,1,3,2:T(8,128)S(1)}, f32[16,3,6,10,128]{4,0,1,3,2:T(8,128)}, u32[]{:S(2)}) copy-start(f32[16,3,6,10,128]{4,0,1,3,2:T(8,128)} %get-tuple-element.65) | copy-start | bytes 4423684
  56.2 2.5 %copy-start.5 = (f32[16,3,6,10,128]{4,0,1,3,2:T(8,128)S(1)}, f32[16,3,6,10,128]{4,0,1,3,2:T(8,128)}, u32[]{:S(2)}) copy-start(f32[16,3,6,10,128]{4,0,1,3,2:T(8,128)} %get-tuple-element.76) | copy-start | bytes 4423684
  58.8 2.1 %copy-start.18 = (f32[16,3,6,10,128]{4,0,1,3,2:T(8,128)S(1)}, f32[16,3,6,10,128]{4,0,1,3,2:T(8,128)}, u32[]{:S(2)}) copy-start(f32[16,3,6,10,128]{4,0,1,3,2:T(8,128)} %get-tuple-element.59) | copy-start | bytes 4423684
  58.8 2.5 %copy-start.19 = (f32[16,3,6,10,128]{4,0,1,3,2:T(8,128)S(1)}, f32[16,3,6,10,128]{4,0,1,3,2:T(8,128)}, u32[]{:S(2)}) copy-start(f32[16,3,6,10,128]{4,0,1,3,2:T(8,128)} %get-tuple-element.78) | copy-start | bytes 4423684
  61.3 2.2 %copy-start.3 = (f32[16,3,6,10,128]{4,0,1,3,2:T(8,128)S(1)}, f32[16,3,6,10,128]{4,0,1,3,2:T(8,128)}, u32[]{:S(2)}) copy-start(f32[16,3,6,10,128]{4,0,1,3,2:T(8,128)} %get-tuple-element.83) | copy-start | bytes 4423684
  61.3 14.6 %copy-start.40 = (f32[16,1,6,10,128]{4,0,1,3,2:T(8,128)S(1)}, f32[16,1,6,10,128]{4,0,1,3,2:T(8,128)}, u32[]{:S(2)}) copy-start(f32[16,1,6,10,128]{4,0,1,3,2:T(8,128)} %get-tuple-element.133) | copy-start | bytes 1474564
  61.3 14.6 %copy-start.41 = (f32[16,1,6,10,128]{4,0,1,3,2:T(8,128)S(1)}, f32[16,1,6,10,128]{4,0,1,3,2:T(8,128)}, u32[]{:S(2)}) copy-start(f32[16,1,6,10,128]{4,0,1,3,2:T(8,128)} %get-tuple-element.134) | copy-start | bytes 1474564
  63.5 2.0 %copy-start.1 = (f32[16,3,6,10,128]{4,0,1,3,2:T(8,128)S(1)}, f32[16,3,6,10,128]{4,0,1,3,2:T(8,128)}, u32[]{:S(2)}) copy-start(f32[16,3,6,10,128]{4,0,1,3,2:T(8,128)} %get-tuple-element.84) | copy-start | bytes 4423684
  63.5 12.4 %copy-start.33 = (f32[16,1,6,10,128]{4,0,1,3,2:T(8,128)S(1)}, f32[16,1,6,10,128]{4,0,1,3,2:T(8,128)}, u32[]{:S(2)}) copy-start(f32[16,1,6,10,128]{4,0,1,3,2:T(8,128)} %get-tuple-element.94) | copy-start | bytes 1474564
  63.5 12.4 %copy-start.34 = (f32[16,1,6,10,128]{4,0,1,3,2:T(8,128)S(1)}, f32[16,1,6,10,128]{4,0,1,3,2:T(8,128)}, u32[]{:S(2)}) copy-start(f32[16,1,6,10,128]{4,0,1,3,2:T(8,128)} %get-tuple-element.41) | copy-start | bytes 1474564
  63.5 12.4 %copy-start.35 = (f32[16,1,6,10,128]{4,0,1,3,2:T(8,128)S(1)}, f32[16,1,6,10,128]{4,0,1,3,2:T(8,128)}, u32[]{:S(2)}) copy-start(f32[16,1,6,10,128]{4,0,1,3,2:T(8,128)} %get-tuple-element.42) | copy-start | bytes 1474564
  63.5 12.4 %copy-start.36 = (f32[16,1,6,10,128]{4,0,1,3,2:T(8,128)S(1)}, f32[16,1,6,10,128]{4,0,1,3,2:T(8,128)}, u32[]{:S(2)}) copy-start(f32[16,1,6,10,128]{4,0,1,3,2:T(8,128)} %get-tuple-element.137) | copy-start | bytes 1474564
  63.5 12.4 %copy-start.37 = (f32[16,1,6,10,128]{4,0,1,3,2:T(8,128)S(1)}, f32[16,1,6,10,128]{4,0,1,3,2:T(8,128)}, u32[]{:S(2)}) copy-start(f32[16,1,6,10,128]{4,0,1,3,2:T(8,128)} %get-tuple-element.95) | copy-start | bytes 1474564
  63.5 12.4 %copy-start.38 = (f32[16,1,6,10,128]{4,0,1,3,2:T(8,128)S(1)}, f32[16,1,6,10,128]{4,0,1,3,2:T(8,128)}, u32[]{:S(2)}) copy-start(f32[16,1,6,10,128]{4,0,1,3,2:T(8,128)} %get-tuple-element.96) | copy-start | bytes 1474564
  63.5 12.4 %copy-start.39 = (f32[16,1,6,10,128]{4,0,1,3,2:T(8,128)S(1)}, f32[16,1,6,10,128]{4,0,1,3,2:T(8,128)}, u32[]{:S(2)}) copy-start(f32[16,1,6,10,128]{4,0,1,3,2:T(8,128)} %get-tuple-element.15) | copy-start | bytes 1474564
  65.5 10.4 %copy-start.23 = (f32[16,1,6,10,128]{4,0,1,3,2:T(8,128)S(1)}, f32[16,1,6,10,128]{4,0,1,3,2:T(8,128)}, u32[]{:S(2)}) copy-start(f32[16,1,6,10,128]{4,0,1,3,2:T(8,128)} %get-tuple-element.90) | copy-start | bytes 1474564
  65.5 10.4 %copy-start.24 = (f32[16,1,6,10,128]{4,0,1,3,2:T(8,128)S(1)}, f32[16,1,6,10,128]{4,0,1,3,2:T(8,128)}, u32[]{:S(2)}) copy-start(f32[16,1,6,10,128]{4,0,1,3,2:T(8,128)} %get-tuple-element.37) | copy-start | bytes 1474564
  65.5 10.4 %copy-start.25 = (f32[16,1,6,10,128]{4,0,1,3,2:T(8,128)S(1)}, f32[16,1,6,10,128]{4,0,1,3,2:T(8,128)}, u32[]{:S(2)}) copy-start(f32[16,1,6,10,128]{4,0,1,3,2:T(8,128)} %get-tuple-element.38) | copy-start | bytes 1474564
  65.5 10.5 %copy-start.26 = (f32[16,1,6,10,128]{4,0,1,3,2:T(8,128)S(1)}, f32[16,1,6,10,128]{4,0,1,3,2:T(8,128)}, u32[]{:S(2)}) copy-start(f32[16,1,6,10,128]{4,0,1,3,2:T(8,128)} %get-tuple-element.149) | copy-start | bytes 1474564
  65.5 10.5 %copy-start.27 = (f32[16,1,6,10,128]{4,0,1,3,2:T(8,128)S(1)}, f32[16,1,6,10,128]{4,0,1,3,2:T(8,128)}, u32[]{:S(2)}) copy-start(f32[16,1,6,10,128]{4,0,1,3,2:T(8,128)} %get-tuple-element.91) | copy-start | bytes 1474564
  65.5 10.5 %copy-start.28 = (f32[16,1,6,10,128]{4,0,1,3,2:T(8,128)S(1)}, f32[16,1,6,10,128]{4,0,1,3,2:T(8,128)}, u32[]{:S(2)}) copy-start(f32[16,1,6,10,128]{4,0,1,3,2:T(8,128)} %get-tuple-element.92) | copy-start | bytes 1474564
  65.5 10.5 %copy-start.29 = (f32[16,1,6,10,128]{4,0,1,3,2:T(8,128)S(1)}, f32[16,1,6,10,128]{4,0,1,3,2:T(8,128)}, u32[]{:S(2)}) copy-start(f32[16,1,6,10,128]{4,0,1,3,2:T(8,128)} %get-tuple-element.11) | copy-start | bytes 1474564
  65.5 10.5 %copy-start.30 = (f32[16,1,6,10,128]{4,0,1,3,2:T(8,128)S(1)}, f32[16,1,6,10,128]{4,0,1,3,2:T(8,128)}, u32[]{:S(2)}) copy-start(f32[16,1,6,10,128]{4,0,1,3,2:T(8,128)} %get-tuple-element.147) | copy-start | bytes 1474564
  65.6 10.5 %copy-start.31 = (f32[16,1,6,10,128]{4,0,1,3,2:T(8,128)S(1)}, f32[16,1,6,10,128]{4,0,1,3,2:T(8,128)}, u32[]{:S(2)}) copy-start(f32[16,1,6,10,128]{4,0,1,3,2:T(8,128)} %get-tuple-element.148) | copy-start | bytes 1474564
  65.6 10.5 %copy-start.32 = (f32[16,1,6,10,128]{4,0,1,3,2:T(8,128)S(1)}, f32[16,1,6,10,128]{4,0,1,3,2:T(8,128)}, u32[]{:S(2)}) copy-start(f32[16,1,6,10,128]{4,0,1,3,2:T(8,128)} %get-tuple-element.93) | copy-start | bytes 1474564
  67.0 9.1 %copy-start.20 = (f32[16,1,6,10,128]{4,0,1,3,2:T(8,128)S(1)}, f32[16,1,6,10,128]{4,0,1,3,2:T(8,128)}, u32[]{:S(2)}) copy-start(f32[16,1,6,10,128]{4,0,1,3,2:T(8,128)} %get-tuple-element.87) | copy-start | bytes 1474564
  67.0 9.1 %copy-start.21 = (f32[16,1,6,10,128]{4,0,1,3,2:T(8,128)S(1)}, f32[16,1,6,10,128]{4,0,1,3,2:T(8,128)}, u32[]{:S(2)}) copy-start(f32[16,1,6,10,128]{4,0,1,3,2:T(8,128)} %get-tuple-element.88) | copy-start | bytes 1474564
  67.0 9.1 %copy-start.22 = (f32[16,1,6,10,128]{4,0,1,3,2:T(8,128)S(1)}, f32[16,1,6,10,128]{4,0,1,3,2:T(8,128)}, u32[]{:S(2)}) copy-start(f32[16,1,6,10,128]{4,0,1,3,2:T(8,128)} %get-tuple-element.89) | copy-start | bytes 1474564
  67.1 2.9 %collective-permute-start.2 = (f32[6,1,128]{2,1,0:T(1,128)S(1)}, f32[6,1,128]{2,1,0:T(1,128)S(1)}, u32[]{:S(2)}, u32[]{:S(2)}) collective-permute-start(f32[6,1,128]{2,1,0:T(1,128)S(1)} %get-tuple-element.127), channel_id=1, source_target_pairs={{0,1},{1,2},{2,3},{4,5},{5,6},{6,7},{8,9},{9,10},{10,11},{12,13},{... | collective-permute-start | bytes 9224 | tf_op jit(solution)/shard_map/ppermute | solution.py:21
  68.6 4.8 %collective-permute-start.3 = (f32[6,1,128]{2,1,0:T(1,128)S(1)}, f32[6,1,128]{2,1,0:T(1,128)S(1)}, u32[]{:S(2)}, u32[]{:S(2)}) collective-permute-start(f32[6,1,128]{2,1,0:T(1,128)S(1)} %get-tuple-element.128), channel_id=1, source_target_pairs={{1,0},{2,1},{3,2},{5,4},{6,5},{7,6},{9,8},{10,9},{11,10},{13,12},{... | collective-permute-start | bytes 9224 | tf_op jit(solution)/shard_map/ppermute | solution.py:23
  95.0 7.3 %collective-permute-start.6 = (f32[16,3,6,1,128]{4,0,1,3,2:T(8,128)S(1)}, f32[16,3,6,1,128]{4,0,1,3,2:T(8,128)S(1)}, u32[]{:S(2)}, u32[]{:S(2)}) collective-permute-start(f32[16,3,6,1,128]{4,0,1,3,2:T(8,128)S(1)} %get-tuple-element.57), channel_id=1, source_target_pairs={{0,1},{1,2},{2,3},{4,5},{5,6},{6,7},{8,9},{9,10},{10,11},{12,13},{... | collective-permute-start | bytes 442376 | tf_op jit(solution)/shard_map/ppermute | solution.py:21
  99.2 3.3 %collective-permute-start.7 = (f32[16,3,6,1,128]{4,0,1,3,2:T(8,128)S(1)}, f32[16,3,6,1,128]{4,0,1,3,2:T(8,128)S(1)}, u32[]{:S(2)}, u32[]{:S(2)}) collective-permute-start(f32[16,3,6,1,128]{4,0,1,3,2:T(8,128)S(1)} %get-tuple-element.58), channel_id=1, source_target_pairs={{1,0},{2,1},{3,2},{5,4},{6,5},{7,6},{9,8},{10,9},{11,10},{13,12},{... | collective-permute-start | bytes 442376 | tf_op jit(solution)/shard_map/ppermute | solution.py:23
  (4 other events, 5.8 us)
Sparse Core Ops, SparseCore 0:
  104.9 24.6 reduce-scatter.1
where the time goes:
time: 137 us
  other arithmetic  56.3 us (41%)
  waiting for transfers between devices  28.5 us (21%)
  starting transfers between devices  20.4 us (15%)
  between operations  14 us (10%)
  local copies, waits for them, and re-layouts  12.9 us (9%)
  matrix products  4.39 us (3%)
    reduce_scatter x1, waiting for transfers between devices, shards(): lax.psum_scatter(partial_value, 'gy', scatter_dimension=0, tiled=True)  24.9 us
    ppermute x4, starting transfers between devices, extended(): lax.ppermute(tail, axis, [(i, (i + 1) % count) for i in range(ends)])  15.3 us
    add x1, other arithmetic, apply_operator(): result = result + coupling * pushed  14.9 us
    sub x2, other arithmetic, apply_operator(): differ = centre - nearby  13.3 us
    unnamed x89, local copies, waits for them, and re-layouts  10.1 us
    mul x6, other arithmetic, apply_operator(): step_y * along_dir  9.16 us
    mul x6, other arithmetic, apply_operator(): beta_shear / reach_len  7.36 us
    mul x6, other arithmetic, apply_operator(): step_x * along_dir  6.87 us
  transfers between devices with their start and end apart: 9, of which 3 were waited for; matrix products, arithmetic and copies ran while one was open for 45% of the time, Pallas kernels for 0%

commit v1 on v0

v1 whole, which is shorter than its diff:
```python
import functools

import jax
import jax.numpy as jnp
from jax import lax
from jax.experimental import pallas as pl
from jax.experimental.pallas import tpu as pltpu
from jax.sharding import PartitionSpec as P

GROUPS = 4

beta_shear = 0.5
mass_share = 0.1

W1, W2, W3 = 0.5, 0.25, 0.125
B1, B2, B3 = W1 * beta_shear, W2 * beta_shear / 2, W3 * beta_shear / 3
DIAG_SUM = 6 * W1 + 12 * W2 + 8 * W3 + 2 * B1 + 8 * B2 + 8 * B3

MESH = pl.DeviceIdType.MESH
RING = [(-1, -1), (-1, 0), (-1, 1), (0, -1), (0, 1), (1, -1), (1, 0), (1, 1)]
HELD = [(1, 0), (0, 1), (1, -1), (1, 1)]


def lane_steps(value):
    lane = lax.broadcasted_iota(jnp.int32, value.shape, value.ndim - 1)
    size = value.shape[-1]
    before = jnp.where(lane == 0, 0.0, pltpu.roll(value, 1, value.ndim - 1))
    after = jnp.where(lane == size - 1, 0.0, pltpu.roll(value, size - 1, value.ndim - 1))
    return before + after, after - before


def plane_parts(fields, low, high):
    span = fields[0].shape[0]

    def at(value, step):
        first, last = low + step, high + step
        start, stop = min(max(first, 0), span), min(max(last, 0), span)
        zeros = lambda n: [jnp.zeros((n,) + value.shape[1:], value.dtype)] if n else []
        if start >= stop:
            return zeros(last - first)[0]
        pieces = zeros(start - first) + [value[start:stop]] + zeros(last - stop)
        return pieces[0] if len(pieces) == 1 else jnp.concatenate(pieces, axis=0)

    def even(value):
        return at(value, -1) + at(value, 1)

    def odd(value):
        return at(value, 1) - at(value, -1)

    vx, vy, vz = fields
    (ex, ox), (ey, oy), (ez, oz) = [lane_steps(v) for v in fields]
    level = at(W1 * ex, 0) + even(W1 * vx + W2 * ex)
    share = at((W1 + B1) * vx + (W2 + B2) * ex, 0) + even((W2 + B2) * vx + (W3 + B3) * ex)
    turn = odd(B2 * vy + B3 * ey) + B2 * at(oz, 0) + B3 * even(oz)
    out_x = (level, share + turn, share - turn)
    skew = odd(oz)
    level = at(W1 * ey, 0) + even((W1 + B1) * vy + (W2 + B2) * ey) + B2 * skew
    share = at(W1 * vy + W2 * ey, 0) + even((W2 + B2) * vy + (W3 + B3) * ey) + B3 * skew
    turn = odd(B2 * vx + B3 * ex)
    out_y = (level, share + turn, share - turn)
    skew = odd(oy)
    wide = W1 * vz + (W2 + B2) * ez
    level = at((W1 + B1) * ez, 0) + even(wide) + B2 * skew
    share = at(wide, 0) + even(W2 * vz + (W3 + B3) * ez) + B3 * skew
    turn = B2 * at(ox, 0) + B3 * even(ox)
    out_z = (level, share + turn, share - turn)
    here, before, after = zip(out_x, out_y, out_z)
    return here, before, after


def stacked(value):
    high = value.astype(jnp.bfloat16)
    low = (value - high.astype(jnp.float32)).astype(jnp.bfloat16)
    cells = value.shape[0]
    join = lambda part: jnp.concatenate([part[i] for i in range(cells)], axis=1)
    return jnp.concatenate([join(high), join(low)], axis=0)


def product(left, right):
    return lax.dot_general(
        left, right, (((1,), (1,)), ((), ())), preferred_element_type=jnp.float32
    )


def folded(value, width):
    value = value[:width] + value[width:]
    return value[:, :width] + value[:, width:]


def kernel(
    shape, counts, modes, region, stiff, group, out,
    field, cells, ring_row, ring_side, ring_corner, sigma, diag,
    halo_x, halo_y, halo_c, part_a, part_b, got_a, got_b,
    load_sem, ring_send, ring_recv, halo_send, halo_recv, a_send, a_recv, b_send, b_recv,
):
    width, span_x, span_y, span_z = shape
    count_x, count_y = counts
    rows = GROUPS * width // count_y
    me_x, me_y = lax.axis_index("gx"), lax.axis_index("gy")

    def exists(step_x, step_y):
        ok = me_x >= 0
        if step_x < 0:
            ok = jnp.logical_and(ok, me_x > 0)
        if step_x > 0:
            ok = jnp.logical_and(ok, me_x < count_x - 1)
        if step_y < 0:
            ok = jnp.logical_and(ok, me_y > 0)
        if step_y > 0:
            ok = jnp.logical_and(ok, me_y < count_y - 1)
        return ok

    def where_is(step_x, step_y):
        return {"gx": me_x + step_x, "gy": me_y + step_y}

    load_modes = pltpu.make_async_copy(modes, field, load_sem.at[0])
    load_region = pltpu.make_async_copy(region, cells, load_sem.at[1])
    load_region.start()
    load_modes.start()

    barrier = pltpu.get_barrier_semaphore()
    for step_x in (-1, 0, 1):
        @pl.when(exists(step_x, 0))
        def _():
            for other in range(1 if step_x == 0 else 0, count_y):
                there = lax.rem(me_y + other, count_y)
                pl.semaphore_signal(
                    barrier, inc=1,
                    device_id={"gx": me_x + step_x, "gy": there}, device_id_type=MESH,
                )
    strips = 1 + (me_x > 0).astype(jnp.int32) + (me_x < count_x - 1).astype(jnp.int32)
    pl.semaphore_wait(barrier, strips * count_y - 1)

    def ring_refs(slot):
        step_x, step_y = RING[slot]
        if step_x == 0:
            return region, ring_side.at[(step_y + 1) // 2]
        plane = region.at[0 if step_x > 0 else span_x - 1]
        if step_y == 0:
            return plane, ring_row.at[(step_x + 1) // 2]
        return plane, ring_corner.at[(step_x + 1) + (step_y + 1) // 2]

    def ring_copy(slot):
        step_x, step_y = RING[slot]
        source, target = ring_refs(slot)
        return pltpu.make_async_remote_copy(
            src_ref=source, dst_ref=target,
            send_sem=ring_send.at[slot], recv_sem=ring_recv.at[slot],
            device_id=where_is(-step_x, -step_y), device_id_type=MESH,
        )

    def halo_copy(slot):
        step_x, step_y = HELD[slot]
        if slot == 0:
            source, target = modes.at[:, 0], halo_x.reshape(3 * width, span_y, span_z)
        elif slot == 1:
            source, target = modes.at[:, :, 0], halo_y
        else:
            source, target = modes.at[:, 0, 0 if step_y > 0 else span_y - 1], halo_c.at[slot - 2]
        return pltpu.make_async_remote_copy(
            src_ref=source, dst_ref=target,
            send_sem=halo_send.at[slot], recv_sem=halo_recv.at[slot],
            device_id=where_is(-step_x, -step_y), device_id_type=MESH,
        )

    for slot, (step_x, step_y) in enumerate(RING):
        @pl.when(exists(-step_x, -step_y))
        def _():
            ring_copy(slot).start()
    for slot, (step_x, step_y) in enumerate(HELD):
        @pl.when(exists(-step_x, -step_y))
        def _():
            halo_copy(slot).start()

    for slot, (step_x, step_y) in enumerate(RING):
        @pl.when(jnp.logical_not(exists(step_x, step_y)))
        def _():
            target = ring_refs(slot)[1]
            target[...] = jnp.full(target.shape, -1, jnp.int32)
    for slot, (step_x, step_y) in enumerate(HELD):
        @pl.when(jnp.logical_not(exists(step_x, step_y)))
        def _():
            if slot == 0:
                halo_x[...] = jnp.zeros(halo_x.shape, jnp.float32)
            elif slot == 1:
                halo_y[...] = jnp.zeros(halo_y.shape, jnp.float32)
            else:
                halo_c[slot - 2] = jnp.zeros(halo_c.shape[1:], jnp.float32)

    def stiff_of(values):
        total = jnp.zeros(values.shape, jnp.float32)
        for level in range(stiff.shape[0]):
            total = jnp.where(values == level, stiff[level], total)
        return total

    load_region.wait()
    for x in range(span_x):
        sigma[1 + x, 1 : 1 + span_y] = stiff_of(cells[x])
    load_modes.wait()
    flat = field.reshape(3 * width * span_x * span_y, span_z)
    columns = 3 * span_x * span_y

    def column(comp, x, y):
        return flat[pl.ds((comp * span_x + x) * span_y + y, width, stride=columns), :]

    def plane(x):
        return [
            jnp.stack([column(comp, x, y) for y in range(span_y)]) for comp in range(3)
        ]

    for slot, (step_x, step_y) in enumerate(RING):
        @pl.when(exists(step_x, step_y))
        def _():
            ring_copy(slot).wait_recv()
    for side, x in ((0, 0), (1, span_x + 1)):
        sigma[x, 1 : 1 + span_y] = stiff_of(ring_row[side])
        low = stiff_of(ring_corner[2 * side])
        sigma[x, 0:1] = low[span_y - 1 : span_y]
        high = stiff_of(ring_corner[2 * side + 1])
        sigma[x, span_y + 1 : span_y + 2] = high[0:1]
    for x in range(span_x):
        low = stiff_of(ring_side[0, x])
        sigma[1 + x, 0:1] = low[span_y - 1 : span_y]
        high = stiff_of(ring_side[1, x])
        sigma[1 + x, span_y + 1 : span_y + 2] = high[0:1]

    def sigma_parts(x):
        level = {}
        for step in (-1, 0, 1):
            s = sigma[x, 1 + step : 1 + step + span_y]
            level[step] = (s,) + lane_steps(s)
        s0, e0, o0 = level[0]
        se, ee, oe = [level[1][i] + level[-1][i] for i in range(3)]
        so, eo, oo = [level[1][i] - level[-1][i] for i in range(3)]
        return s0, e0, o0, se, ee, oe, so, eo, oo

    parts = [sigma_parts(x) for x in range(span_x + 2)]
    for x in range(1, span_x + 1):
        s0, e0, o0, se, ee, oe, so, eo, oo = parts[x]
        fs, fe, fo, fse, fee, foe, fso, feo, foo = [
            parts[x + 1][i] + parts[x - 1][i] for i in range(9)
        ]
        ds, de, do, dse, dee, doe, dso, deo, doo = [
            parts[x + 1][i] - parts[x - 1][i] for i in range(9)
        ]
        plain = (
            (mass_share + DIAG_SUM) * s0
            + W1 * (e0 + se + fs) + W2 * (ee + fe + fse) + W3 * fee
        )
        xx = plain + B1 * fs + B2 * (fse + fe) + B3 * fee
        yy = plain + B1 * se + B2 * (fse + ee) + B3 * fee
        zz = plain + B1 * e0 + B2 * (fe + ee) + B3 * fee
        xy = B2 * dso + B3 * deo
        xz = B2 * do + B3 * doe
        yz = B2 * oo + B3 * foo
        for i, value in enumerate((xx, yy, zz, xy, xz, yz)):
            diag[i, x - 1] = 0.5 * value

    def spread(row):
        return jnp.broadcast_to(row, (width, span_z))

    def spread_sigma(x, low, high):
        return jnp.stack([spread(sigma[1 + x, 1 + y : 2 + y]) for y in range(low, high)])

    def spread_diag(i, x):
        return jnp.stack([spread(diag[i, x, y : y + 1]) for y in range(span_y)])

    own = jnp.zeros((2 * width, 2 * width), jnp.float32)
    here, before, after, fields, weights = [], [], [], [], []
    edge_here, edge_before, edge_after = [], [], []
    for x in range(span_x):
        last = x == span_x - 1
        v = plane(x)
        s = spread_sigma(x, 0, span_y)
        a, b, c = plane_parts(v, -1 if last else 0, span_y + 1)
        if last:
            beyond = c
            a, b = [[t[1:] for t in group_] for group_ in (a, b)]
            sv = [s * t for t in v]
            ea, eb, ec = plane_parts(sv, -1, span_y + 1)
            beyond_s = ec
            ea, eb = [[t[span_y + 1 :] for t in group_] for group_ in (ea, eb)]
        else:
            sv = [s[span_y - 1 :] * t[span_y - 1 :] for t in v]
            ea, eb, ec = plane_parts(sv, 1, 2)
        here.append(a); before.append(b); after.append(c)
        edge_here.append(ea); edge_before.append(eb); edge_after.append(ec)
        fields.append(v); weights.append(s)

    side = []
    for x in range(span_x):
        reach = list(here[x])
        edge = list(edge_here[x])
        if x + 1 < span_x:
            reach = [r + t for r, t in zip(reach, before[x + 1])]
            edge = [r + t for r, t in zip(edge, edge_before[x + 1])]
        if x > 0:
            reach = [r + t for r, t in zip(reach, after[x - 1])]
            edge = [r + t for r, t in zip(edge, edge_after[x - 1])]
        v, s = fields[x], weights[x]
        dxx, dyy, dzz, dxy, dxz, dyz = [spread_diag(i, x) for i in range(6)]
        applied = [
            dxx * v[0] + dxy * v[1] + dxz * v[2],
            dxy * v[0] + dyy * v[1] + dyz * v[2],
            dxz * v[0] + dyz * v[1] + dzz * v[2],
        ]
        for comp in range(3):
            left = applied[comp] - s * reach[comp][:span_y]
            own = own + product(stacked(left), stacked(v[comp]))
        s_side = spread_sigma(x, span_y, span_y + 1)
        side.append([stacked(s_side * reach[i][span_y:] + edge[i]) for i in range(3)])
    s_row = spread_sigma(span_x, -1, span_y + 1)
    row = [s_row * beyond[i] + beyond_s[i] for i in range(3)]
    row_mid = [stacked(t[1 : span_y + 1]) for t in row]
    row_low = [stacked(t[:1]) for t in row]
    row_high = [stacked(t[span_y + 1 :]) for t in row]
    block = folded(own, width)
    block = block + block.T

    for slot, (step_x, step_y) in enumerate(HELD):
        @pl.when(exists(step_x, step_y))
        def _():
            halo_copy(slot).wait_recv()

    def pair(left, right):
        total = product(left[0], right[0])
        for l, r in zip(left[1:], right[1:]):
            total = total + product(l, r)
        return -folded(total, width)

    flat_y = halo_y.reshape(3 * width * span_x, span_z)
    near_c = [
        [stacked(halo_c[i, pl.ds(comp, width, stride=3), :][None]) for comp in range(3)]
        for i in range(2)
    ]
    c_low = pair(row_low, near_c[0])
    c_high = pair(row_high, near_c[1])
    c_side = pair(
        [side[x][comp] for x in range(span_x) for comp in range(3)],
        [
            stacked(flat_y[pl.ds(comp * span_x + x, width, stride=3 * span_x), :][None])
            for x in range(span_x) for comp in range(3)
        ],
    )
    c_mid = pair(
        row_mid,
        [
            stacked(jnp.stack([
                halo_x[pl.ds(comp * span_y + y, width, stride=3 * span_y), :]
                for y in range(span_y)
            ]))
            for comp in range(3)
        ],
    )

    next_x = jnp.minimum(me_x + 1, count_x - 1)
    next_y = jnp.minimum(me_y + 1, count_y - 1)
    last_y = jnp.maximum(me_y - 1, 0)
    g_self, g_side = group[me_x, me_y], group[me_x, next_y]
    g_low, g_mid, g_high = group[next_x, last_y], group[next_x, me_y], group[next_x, next_y]
    slot_of = lax.broadcasted_iota(jnp.int32, (width, GROUPS * width), 1) // width

    def placed(value, label):
        return jnp.where(slot_of == label, jnp.concatenate([value] * GROUPS, axis=1), 0.0)

    level = placed(block, g_self) + placed(c_side, g_side)
    ahead = placed(c_low, g_low) + placed(c_mid, g_mid) + placed(c_high, g_high)
    strip = jnp.concatenate([level, ahead], axis=1)
    none = jnp.zeros_like(level)
    back_side = jnp.concatenate([placed(c_side.T, g_self), none], axis=1)
    backs = [
        (jnp.concatenate([placed(value.T, g_self), none], axis=1), label)
        for value, label in ((c_low, g_low), (c_mid, g_mid), (c_high, g_high))
    ]
    for g in range(GROUPS):
        part_a[g * width : (g + 1) * width] = (
            jnp.where(g_self == g, strip, 0.0) + jnp.where(g_side == g, back_side, 0.0)
        )
        total = jnp.zeros_like(strip)
        for value, label in backs:
            total = total + jnp.where(label == g, value, 0.0)
        part_b[g * width : (g + 1) * width] = total

    def rows_of(there):
        return pl.ds(pl.multiple_of(there * rows, rows), rows)

    def a_copy(other):
        there = lax.rem(me_y + other, count_y)
        return pltpu.make_async_remote_copy(
            src_ref=part_a.at[rows_of(there)], dst_ref=got_a.at[other],
            send_sem=a_send.at[other], recv_sem=a_recv.at[other],
            device_id={"gx": me_x, "gy": there}, device_id_type=MESH,
        )

    def b_copy(other):
        there = lax.rem(me_y + other, count_y)
        return pltpu.make_async_remote_copy(
            src_ref=part_b.at[rows_of(there)], dst_ref=got_b.at[other],
            send_sem=b_send.at[other], recv_sem=b_recv.at[other],
            device_id={"gx": me_x + 1, "gy": there}, device_id_type=MESH,
        )

    @pl.when(exists(1, 0))
    def _():
        for other in range(count_y):
            b_copy(other).start()

    for other in range(1, count_y):
        a_copy(other).start()

    @pl.when(jnp.logical_not(exists(-1, 0)))
    def _():
        got_b[...] = jnp.zeros(got_b.shape, jnp.float32)

    total = part_a[rows_of(me_y), :]
    for other in range(1, count_y):
        a_copy(other).wait_recv()
        total = total + got_a[other]
    out[0, :, GROUPS * width :] = total

    @pl.when(exists(-1, 0))
    def _():
        for other in range(count_y):
            b_copy(other).wait_recv()

    total = got_b[0]
    for other in range(1, count_y):
        total = total + got_b[other]
    out[0, :, : GROUPS * width] = total[:, : GROUPS * width]

    for slot, (step_x, step_y) in enumerate(RING):
        @pl.when(exists(-step_x, -step_y))
        def _():
            ring_copy(slot).wait_send()
    for slot, (step_x, step_y) in enumerate(HELD):
        @pl.when(exists(-step_x, -step_y))
        def _():
            halo_copy(slot).wait_send()
    for other in range(1, count_y):
        a_copy(other).wait_send()

    @pl.when(exists(1, 0))
    def _():
        for other in range(count_y):
            b_copy(other).wait_send()


def shards(counts, modes, region, stiffness, coarse_group):
    width, comps, span_x, span_y, span_z = modes.shape
    rows = GROUPS * width // counts[1]
    f32, i32 = jnp.float32, jnp.int32
    dma = pltpu.SemaphoreType.DMA
    lanes = 2 * GROUPS * width
    return pl.pallas_call(
        functools.partial(kernel, (width, span_x, span_y, span_z), counts),
        out_shape=jax.ShapeDtypeStruct((1, rows, 3 * GROUPS * width), f32),
        in_specs=[
            pl.BlockSpec(memory_space=pl.ANY),
            pl.BlockSpec(memory_space=pl.ANY),
            pl.BlockSpec(memory_space=pltpu.SMEM),
            pl.BlockSpec(memory_space=pltpu.SMEM),
        ],
        out_specs=pl.BlockSpec(memory_space=pltpu.VMEM),
        scratch_shapes=[
            pltpu.VMEM((comps * width, span_x, span_y, span_z), f32),
            pltpu.VMEM((span_x, span_y, span_z), i32),
            pltpu.VMEM((2, span_y, span_z), i32),
            pltpu.VMEM((2, span_x, span_y, span_z), i32),
            pltpu.VMEM((4, span_y, span_z), i32),
            pltpu.VMEM((span_x + 2, span_y + 8, span_z), f32),
            pltpu.VMEM((6, span_x, span_y, span_z), f32),
            pltpu.VMEM((comps * width * span_y, span_z), f32),
            pltpu.VMEM((comps * width, span_x, span_z), f32),
            pltpu.VMEM((2, comps * width, span_z), f32),
            pltpu.VMEM((GROUPS * width, lanes), f32),
            pltpu.VMEM((GROUPS * width, lanes), f32),
            pltpu.VMEM((counts[1], rows, lanes), f32),
            pltpu.VMEM((counts[1], rows, lanes), f32),
            dma((2,)),
            dma((len(RING),)), dma((len(RING),)),
            dma((len(HELD),)), dma((len(HELD),)),
            dma((counts[1],)), dma((counts[1],)),
            dma((counts[1],)), dma((counts[1],)),
        ],
        compiler_params=pltpu.CompilerParams(collective_id=0, has_side_effects=True),
    )(modes.reshape(width * comps, span_x, span_y, span_z), region, stiffness, coarse_group)


def solution(mesh):
    counts = (mesh.shape["gx"], mesh.shape["gy"])
    in_specs = (P(None, None, "gx", "gy", None), P("gx", "gy", None), P(), P())
    out_specs = P("gx", "gy", None)
    return jax.shard_map(
        functools.partial(shards, counts), mesh=mesh, in_specs=in_specs,
        out_specs=out_specs, check_vma=False,
    )
```

time: 137 us -> 19.6 us (0.14)
  other arithmetic: 56.3 us -> 0 us
  waiting for transfers between devices: 28.5 us -> 0 us
  starting transfers between devices: 20.4 us -> 0 us
  Pallas kernels: 0 us -> 16.6 us
  between operations: 14 us -> 0.01 us
  local copies, waits for them, and re-layouts: 12.9 us -> 2.67 us
  matrix products: 4.39 us -> 0 us
    mul x21 -> x0, other arithmetic: 25.8 us -> none  [the longest x6 9.16 us: apply_operator(): step_y * along_dir]
    reduce_scatter x1 -> x0, waiting for transfers between devices: 24.9 us -> none  [shards(): lax.psum_scatter(partial_value, 'gy', scatter_dimension=0, tiled=True)]
    ppermute x8 -> x0, starting transfers between devices: 20.4 us -> none  [the longest x4 15.3 us: extended(): lax.ppermute(tail, axis, [(i, (i + 1) % count) for i in range(ends)])]
    pallas_call x0 -> x1, Pallas kernels: none -> 16.6 us  [shards(): pl.pallas_call(functools.partial(kernel, (width, span_x, span_y, span_z),...]
    add x1 -> x0, other arithmetic: 14.9 us -> none  [apply_operator(): result = result + coupling * pushed]
    sub x2 -> x0, other arithmetic: 13.3 us -> none  [apply_operator(): differ = centre - nearby]
    unnamed x89 -> x2, local copies, waits for them, and re-layouts: 10.1 us -> 2.67 us
    dot_general x10 -> x0, matrix products: 4.39 us -> none  [the longest x9 4.11 us: contract(): jnp.einsum('kaxyz,jaxyz->kj', left_side, right_side, precision=lax.Precis...]
  transfers between devices with their start and end apart: 9 -> 0, of which waited for: 3 -> 0; matrix products, arithmetic and copies ran while one was open for 45% -> 0% of each run, Pallas kernels for 0% -> 0%
where the time goes in v1:
time: 19.6 us; the launch traced here: 19.2 us
  Pallas kernels  16.6 us (85%)
  local copies, waits for them, and re-layouts  2.67 us (14%)
    pallas_call x1, Pallas kernels, shards(): pl.pallas_call(functools.partial(kernel, (width, span_x, span_y, span_z),...  16.6 us
    unnamed x2, local copies, waits for them, and re-layouts  2.67 us

profile of v1, /device:TPU:0, one launch (start us, length us, event | category | flops | bytes accessed | tf_op | source)
XLA Modules:
  0.0 19.2 jit_solution(8564931539923065104)
XLA Ops:
  0.0 1.3 %copy.5.group = s32[8,4]{1,0:T(8,128)} copy(s32[8,4]{0,1:T(4,128)} %param.7) | data formatting | bytes 256 | tf_op args[3]
  1.3 16.6 %shard_map.46 = f32[1,16,192]{2,1,0:T(8,128)} custom-call(f32[48,4,8,128]{3,2,1,0:T(8,128)} %bitcast.1, s32[4,8,128]{2,1,0:T(8,128)} %region.1, f32[16]{0:T(128)} %stiff.1, s32[8,4]{1,0:T(8,128)} %copy.5.group), custom_call_target="tpu_custom_call" | custom-call | tf_op jit(solution)/shard_map/pallas_call | solution.py:454
  17.9 1.3 %copy.7 = f32[1,16,192]{2,1,0:T(8,128)} copy(f32[1,16,192]{2,1,0:T(8,128)} %shard_map.46) | data formatting | bytes 24576

commit v2 on v1

--- a/solution.py
+++ b/solution.py
@@ -18,7 +18,7 @@
 
 MESH = pl.DeviceIdType.MESH
 RING = [(-1, -1), (-1, 0), (-1, 1), (0, -1), (0, 1), (1, -1), (1, 0), (1, 1)]
-HELD = [(1, 0), (0, 1), (1, -1), (1, 1)]
+HELD = [(1, -1), (1, 1), (0, 1), (1, 0), (1, 0), (1, 0)]
 
 
 def lane_steps(value):
@@ -88,8 +88,8 @@
 
 
 def kernel(
-    shape, counts, modes, region, stiff, group, out,
-    field, cells, ring_row, ring_side, ring_corner, sigma, diag,
+    shape, counts, modes, region, stiff_in, group_in, out,
+    stiff, group, field, cells, ring_row, ring_side, ring_corner, sigma, diag,
     halo_x, halo_y, halo_c, part_a, part_b, got_a, got_b,
     load_sem, ring_send, ring_recv, halo_send, halo_recv, a_send, a_recv, b_send, b_recv,
 ):
@@ -115,8 +115,8 @@
 
     load_modes = pltpu.make_async_copy(modes, field, load_sem.at[0])
     load_region = pltpu.make_async_copy(region, cells, load_sem.at[1])
-    load_region.start()
-    load_modes.start()
+    load_stiff = pltpu.make_async_copy(stiff_in, stiff, load_sem.at[2])
+    load_group = pltpu.make_async_copy(group_in, group, load_sem.at[3])
 
     barrier = pltpu.get_barrier_semaphore()
     for step_x in (-1, 0, 1):
@@ -128,17 +128,22 @@
                     barrier, inc=1,
                     device_id={"gx": me_x + step_x, "gy": there}, device_id_type=MESH,
                 )
+    load_region.start()
+    load_stiff.start()
+    load_group.start()
+    load_modes.start()
     strips = 1 + (me_x > 0).astype(jnp.int32) + (me_x < count_x - 1).astype(jnp.int32)
     pl.semaphore_wait(barrier, strips * count_y - 1)
 
     def ring_refs(slot):
         step_x, step_y = RING[slot]
+        edge_x = 0 if step_x > 0 else span_x - 1
+        edge_y = 0 if step_y > 0 else span_y - 1
         if step_x == 0:
-            return region, ring_side.at[(step_y + 1) // 2]
-        plane = region.at[0 if step_x > 0 else span_x - 1]
+            return region.at[:, edge_y], ring_side.at[(step_y + 1) // 2]
         if step_y == 0:
-            return plane, ring_row.at[(step_x + 1) // 2]
-        return plane, ring_corner.at[(step_x + 1) + (step_y + 1) // 2]
+            return region.at[edge_x], ring_row.at[(step_x + 1) // 2]
+        return region.at[edge_x, edge_y], ring_corner.at[(step_x + 1) + (step_y + 1) // 2]
 
     def ring_copy(slot):
         step_x, step_y = RING[slot]
@@ -151,12 +156,13 @@
 
     def halo_copy(slot):
         step_x, step_y = HELD[slot]
-        if slot == 0:
-            source, target = modes.at[:, 0], halo_x.reshape(3 * width, span_y, span_z)
-        elif slot == 1:
-            source, target = modes.at[:, :, 0], halo_y
+        if slot < 2:
+            merged = modes.reshape(3 * width, span_x, span_y, span_z)
+            source, target = merged.at[:, 0, 0 if step_y > 0 else span_y - 1], halo_c.at[slot]
+        elif slot == 2:
+            source, target = modes.at[:, :, :, 0], halo_y
         else:
-            source, target = modes.at[:, 0, 0 if step_y > 0 else span_y - 1], halo_c.at[slot - 2]
+            source, target = modes.at[:, slot - 3, 0], halo_x.at[slot - 3]
         return pltpu.make_async_remote_copy(
             src_ref=source, dst_ref=target,
             send_sem=halo_send.at[slot], recv_sem=halo_recv.at[slot],
@@ -180,12 +186,8 @@
     for slot, (step_x, step_y) in enumerate(HELD):
         @pl.when(jnp.logical_not(exists(step_x, step_y)))
         def _():
-            if slot == 0:
-                halo_x[...] = jnp.zeros(halo_x.shape, jnp.float32)
-            elif slot == 1:
-                halo_y[...] = jnp.zeros(halo_y.shape, jnp.float32)
-            else:
-                halo_c[slot - 2] = jnp.zeros(halo_c.shape[1:], jnp.float32)
+            target = halo_c.at[slot] if slot < 2 else halo_y if slot == 2 else halo_x.at[slot - 3]
+            target[...] = jnp.zeros(target.shape, jnp.float32)
 
     def stiff_of(values):
         total = jnp.zeros(values.shape, jnp.float32)
@@ -193,6 +195,8 @@
             total = jnp.where(values == level, stiff[level], total)
         return total
 
+    load_stiff.wait()
+    load_group.wait()
     load_region.wait()
     for x in range(span_x):
         sigma[1 + x, 1 : 1 + span_y] = stiff_of(cells[x])
@@ -214,15 +218,12 @@
             ring_copy(slot).wait_recv()
     for side, x in ((0, 0), (1, span_x + 1)):
         sigma[x, 1 : 1 + span_y] = stiff_of(ring_row[side])
-        low = stiff_of(ring_corner[2 * side])
-        sigma[x, 0:1] = low[span_y - 1 : span_y]
-        high = stiff_of(ring_corner[2 * side + 1])
-        sigma[x, span_y + 1 : span_y + 2] = high[0:1]
+        sigma[x, 0:1] = stiff_of(ring_corner[2 * side : 2 * side + 1])
+        sigma[x, span_y + 1 : span_y + 2] = stiff_of(ring_corner[2 * side + 1 : 2 * side + 2])
+    low, high = stiff_of(ring_side[0]), stiff_of(ring_side[1])
     for x in range(span_x):
-        low = stiff_of(ring_side[0, x])
-        sigma[1 + x, 0:1] = low[span_y - 1 : span_y]
-        high = stiff_of(ring_side[1, x])
-        sigma[1 + x, span_y + 1 : span_y + 2] = high[0:1]
+        sigma[1 + x, 0:1] = low[x : x + 1]
+        sigma[1 + x, span_y + 1 : span_y + 2] = high[x : x + 1]
 
     def sigma_parts(x):
         level = {}
@@ -317,8 +318,8 @@
     block = folded(own, width)
     block = block + block.T
 
-    for slot, (step_x, step_y) in enumerate(HELD):
-        @pl.when(exists(step_x, step_y))
+    def arrived(slot):
+        @pl.when(exists(*HELD[slot]))
         def _():
             halo_copy(slot).wait_recv()
 
@@ -326,38 +327,37 @@
         total = product(left[0], right[0])
         for l, r in zip(left[1:], right[1:]):
             total = total + product(l, r)
-        return -folded(total, width)
-
+        return total
+
+    def corner(i):
+        return [stacked(halo_c[i, pl.ds(comp, width, stride=3), :][None]) for comp in range(3)]
+
+    arrived(2)
     flat_y = halo_y.reshape(3 * width * span_x, span_z)
-    near_c = [
-        [stacked(halo_c[i, pl.ds(comp, width, stride=3), :][None]) for comp in range(3)]
-        for i in range(2)
-    ]
-    c_low = pair(row_low, near_c[0])
-    c_high = pair(row_high, near_c[1])
-    c_side = pair(
+    c_side = -folded(pair(
         [side[x][comp] for x in range(span_x) for comp in range(3)],
         [
             stacked(flat_y[pl.ds(comp * span_x + x, width, stride=3 * span_x), :][None])
             for x in range(span_x) for comp in range(3)
         ],
-    )
-    c_mid = pair(
-        row_mid,
-        [
-            stacked(jnp.stack([
-                halo_x[pl.ds(comp * span_y + y, width, stride=3 * span_y), :]
-                for y in range(span_y)
-            ]))
-            for comp in range(3)
-        ],
-    )
+    ), width)
+    arrived(0)
+    c_low = -folded(pair(row_low, corner(0)), width)
+    arrived(1)
+    c_high = -folded(pair(row_high, corner(1)), width)
+    c_mid = jnp.zeros((2 * width, 2 * width), jnp.float32)
+    for comp in range(3):
+        arrived(3 + comp)
+        flat_x = halo_x.at[comp].reshape(width * span_y, span_z)
+        near = jnp.stack([flat_x[pl.ds(y, width, stride=span_y), :] for y in range(span_y)])
+        c_mid = c_mid + product(row_mid[comp], stacked(near))
+    c_mid = -folded(c_mid, width)
 
     next_x = jnp.minimum(me_x + 1, count_x - 1)
     next_y = jnp.minimum(me_y + 1, count_y - 1)
     last_y = jnp.maximum(me_y - 1, 0)
-    g_self, g_side = group[me_x, me_y], group[me_x, next_y]
-    g_low, g_mid, g_high = group[next_x, last_y], group[next_x, me_y], group[next_x, next_y]
+    g_self, g_side = group[me_y, me_x], group[next_y, me_x]
+    g_low, g_mid, g_high = group[last_y, next_x], group[me_y, next_x], group[next_y, next_x]
     slot_of = lax.broadcasted_iota(jnp.int32, (width, GROUPS * width), 1) // width
 
     def placed(value, label):
@@ -455,35 +455,37 @@
         functools.partial(kernel, (width, span_x, span_y, span_z), counts),
         out_shape=jax.ShapeDtypeStruct((1, rows, 3 * GROUPS * width), f32),
         in_specs=[
-            pl.BlockSpec(memory_space=pl.ANY),
-            pl.BlockSpec(memory_space=pl.ANY),
-            pl.BlockSpec(memory_space=pltpu.SMEM),
-            pl.BlockSpec(memory_space=pltpu.SMEM),
+            pl.BlockSpec(memory_space=pltpu.HBM),
+            pl.BlockSpec(memory_space=pltpu.HBM),
+            pl.BlockSpec(memory_space=pltpu.HBM),
+            pl.BlockSpec(memory_space=pltpu.HBM),
         ],
         out_specs=pl.BlockSpec(memory_space=pltpu.VMEM),
         scratch_shapes=[
-            pltpu.VMEM((comps * width, span_x, span_y, span_z), f32),
+            pltpu.SMEM(stiffness.shape, f32),
+            pltpu.SMEM(coarse_group.shape[::-1], i32),
+            pltpu.VMEM((width, comps, span_x, span_y, span_z), f32),
             pltpu.VMEM((span_x, span_y, span_z), i32),
             pltpu.VMEM((2, span_y, span_z), i32),
-            pltpu.VMEM((2, span_x, span_y, span_z), i32),
-            pltpu.VMEM((4, span_y, span_z), i32),
+            pltpu.VMEM((2, span_x, span_z), i32),
+            pltpu.VMEM((4, span_z), i32),
             pltpu.VMEM((span_x + 2, span_y + 8, span_z), f32),
             pltpu.VMEM((6, span_x, span_y, span_z), f32),
-            pltpu.VMEM((comps * width * span_y, span_z), f32),
-            pltpu.VMEM((comps * width, span_x, span_z), f32),
+            pltpu.VMEM((comps, width, span_y, span_z), f32),
+            pltpu.VMEM((width, comps, span_x, span_z), f32),
             pltpu.VMEM((2, comps * width, span_z), f32),
             pltpu.VMEM((GROUPS * width, lanes), f32),
             pltpu.VMEM((GROUPS * width, lanes), f32),
             pltpu.VMEM((counts[1], rows, lanes), f32),
             pltpu.VMEM((counts[1], rows, lanes), f32),
-            dma((2,)),
+            dma((4,)),
             dma((len(RING),)), dma((len(RING),)),
             dma((len(HELD),)), dma((len(HELD),)),
             dma((counts[1],)), dma((counts[1],)),
             dma((counts[1],)), dma((counts[1],)),
         ],
         compiler_params=pltpu.CompilerParams(collective_id=0, has_side_effects=True),
-    )(modes.reshape(width * comps, span_x, span_y, span_z), region, stiffness, coarse_group)
+    )(modes, region, stiffness, coarse_group.T)
 
 
 def solution(mesh):

time: 19.6 us -> 17.3 us (0.88)
  local copies, waits for them, and re-layouts: 2.67 us -> 1.32 us
  Pallas kernels: 16.6 us -> 15.7 us
    unnamed x2 -> x1, local copies, waits for them, and re-layouts: 2.67 us -> 1.32 us
    pallas_call x1, Pallas kernels: 16.6 us -> 15.7 us  [shards(): pl.pallas_call(functools.partial(kernel, (width, span_x, span_y, span_z),...]
where the time goes in v2:
time: 17.3 us; the launch traced here: 17.1 us
  Pallas kernels  15.7 us (91%)
  local copies, waits for them, and re-layouts  1.32 us (8%)
    pallas_call x1, Pallas kernels, shards(): pl.pallas_call(functools.partial(kernel, (width, span_x, span_y, span_z),...  15.7 us
    unnamed x1, local copies, waits for them, and re-layouts  1.32 us

profile of v2, /device:TPU:0, one launch (start us, length us, event | category | flops | bytes accessed | tf_op | source)
XLA Modules:
  0.0 17.1 jit_solution(13971766312188962843)
XLA Ops:
  0.0 15.7 %shard_map.46 = f32[1,16,192]{2,1,0:T(8,128)} custom-call(f32[16,3,4,8,128]{4,3,2,1,0:T(8,128)} %modes.1, s32[4,8,128]{2,1,0:T(8,128)} %region.1, f32[16]{0:T(128)} %stiff_in.1, s32[4,8]{1,0:T(4,128)} %bitcast.1), custom_call_target="tpu_custom_call" | custom-call | tf_op jit(solution)/shard_map/pallas_call | solution.py:454
  15.7 1.3 %copy.6 = f32[1,16,192]{2,1,0:T(8,128)} copy(f32[1,16,192]{2,1,0:T(8,128)} %shard_map.46) | data formatting | bytes 24576

commit v3 on v2

--- a/solution.py
+++ b/solution.py
@@ -453,7 +453,7 @@
     lanes = 2 * GROUPS * width
     return pl.pallas_call(
         functools.partial(kernel, (width, span_x, span_y, span_z), counts),
-        out_shape=jax.ShapeDtypeStruct((1, rows, 3 * GROUPS * width), f32),
+        out_shape=pltpu.VMEM((1, rows, 3 * GROUPS * width), f32),
         in_specs=[
             pl.BlockSpec(memory_space=pltpu.HBM),
             pl.BlockSpec(memory_space=pltpu.HBM),

time: 17.3 us -> 15.9 us (0.919)
  local copies, waits for them, and re-layouts: 1.32 us -> 0.61 us
  Pallas kernels: 15.7 us -> 15.1 us
    unnamed x1, local copies, waits for them, and re-layouts: 1.32 us -> 0.61 us
    pallas_call x1, Pallas kernels: 15.7 us -> 15.1 us  [shards(): pl.pallas_call(functools.partial(kernel, (width, span_x, span_y, span_z),...]
where the time goes in v3:
time: 15.9 us; the launch traced here: 15.8 us
  Pallas kernels  15.1 us (95%)
  local copies, waits for them, and re-layouts  0.61 us (4%)
    pallas_call x1, Pallas kernels, shards(): pl.pallas_call(functools.partial(kernel, (width, span_x, span_y, span_z),...  15.1 us
    unnamed x1, local copies, waits for them, and re-layouts  0.61 us

profile of v3, /device:TPU:0, one launch (start us, length us, event | category | flops | bytes accessed | tf_op | source)
XLA Modules:
  0.0 15.8 jit_solution(1585336077009432100)
XLA Ops:
  0.0 15.1 %shard_map.46 = f32[1,16,192]{2,1,0:T(8,128)S(1)} custom-call(f32[16,3,4,8,128]{4,3,2,1,0:T(8,128)} %modes.1, s32[4,8,128]{2,1,0:T(8,128)} %region.1, f32[16]{0:T(128)} %stiff_in.1, s32[4,8]{1,0:T(4,128)} %bitcast.1), custom_call_target="tpu_custom_call" | custom-call | tf_op jit(solution)/shard_map/pallas_call | solution.py:454
  15.2 0.6 %copy.6 = f32[1,16,192]{2,1,0:T(8,128)} copy(f32[1,16,192]{2,1,0:T(8,128)S(1)} %shard_map.46) | data formatting | bytes 24576

commit v4 on v3

--- a/solution.py
+++ b/solution.py
@@ -345,6 +345,49 @@
     c_low = -folded(pair(row_low, corner(0)), width)
     arrived(1)
     c_high = -folded(pair(row_high, corner(1)), width)
+    next_x = jnp.minimum(me_x + 1, count_x - 1)
+    next_y = jnp.minimum(me_y + 1, count_y - 1)
+    last_y = jnp.maximum(me_y - 1, 0)
+    g_self, g_side = group[me_y, me_x], group[next_y, me_x]
+    g_low, g_mid, g_high = group[last_y, next_x], group[me_y, next_x], group[next_y, next_x]
+    slot_of = lax.broadcasted_iota(jnp.int32, (width, GROUPS * width), 1) // width
+
+    def placed(value, label):
+        return jnp.where(slot_of == label, jnp.concatenate([value] * GROUPS, axis=1), 0.0)
+
+    level = placed(block, g_self) + placed(c_side, g_side)
+    ahead = placed(c_low, g_low) + placed(c_high, g_high)
+    none = jnp.zeros_like(level)
+    back_side = jnp.concatenate([placed(c_side.T, g_self), none], axis=1)
+    back_low, back_high = placed(c_low.T, g_self), placed(c_high.T, g_self)
+    backs = [
+        jnp.where(g_low == g, back_low, 0.0) + jnp.where(g_high == g, back_high, 0.0)
+        for g in range(GROUPS)
+    ]
+
+    @pl.when(jnp.logical_not(exists(-1, 0)))
+    def _():
+        got_b[...] = jnp.zeros(got_b.shape, jnp.float32)
+
+    def rows_of(there):
+        return pl.ds(pl.multiple_of(there * rows, rows), rows)
+
+    def a_copy(other):
+        there = lax.rem(me_y + other, count_y)
+        return pltpu.make_async_remote_copy(
+            src_ref=part_a.at[rows_of(there)], dst_ref=got_a.at[other],
+            send_sem=a_send.at[other], recv_sem=a_recv.at[other],
+            device_id={"gx": me_x, "gy": there}, device_id_type=MESH,
+        )
+
+    def b_copy(other):
+        there = lax.rem(me_y + other, count_y)
+        return pltpu.make_async_remote_copy(
+            src_ref=part_b.at[there], dst_ref=got_b.at[other],
+            send_sem=b_send.at[other], recv_sem=b_recv.at[other],
+            device_id={"gx": me_x + 1, "gy": there}, device_id_type=MESH,
+        )
+
     c_mid = jnp.zeros((2 * width, 2 * width), jnp.float32)
     for comp in range(3):
         arrived(3 + comp)
@@ -353,51 +396,15 @@
         c_mid = c_mid + product(row_mid[comp], stacked(near))
     c_mid = -folded(c_mid, width)
 
-    next_x = jnp.minimum(me_x + 1, count_x - 1)
-    next_y = jnp.minimum(me_y + 1, count_y - 1)
-    last_y = jnp.maximum(me_y - 1, 0)
-    g_self, g_side = group[me_y, me_x], group[next_y, me_x]
-    g_low, g_mid, g_high = group[last_y, next_x], group[me_y, next_x], group[next_y, next_x]
-    slot_of = lax.broadcasted_iota(jnp.int32, (width, GROUPS * width), 1) // width
-
-    def placed(value, label):
-        return jnp.where(slot_of == label, jnp.concatenate([value] * GROUPS, axis=1), 0.0)
-
-    level = placed(block, g_self) + placed(c_side, g_side)
-    ahead = placed(c_low, g_low) + placed(c_mid, g_mid) + placed(c_high, g_high)
-    strip = jnp.concatenate([level, ahead], axis=1)
-    none = jnp.zeros_like(level)
-    back_side = jnp.concatenate([placed(c_side.T, g_self), none], axis=1)
-    backs = [
-        (jnp.concatenate([placed(value.T, g_self), none], axis=1), label)
-        for value, label in ((c_low, g_low), (c_mid, g_mid), (c_high, g_high))
-    ]
-    for g in range(GROUPS):
-        part_a[g * width : (g + 1) * width] = (
-            jnp.where(g_self == g, strip, 0.0) + jnp.where(g_side == g, back_side, 0.0)
-        )
-        total = jnp.zeros_like(strip)
-        for value, label in backs:
-            total = total + jnp.where(label == g, value, 0.0)
-        part_b[g * width : (g + 1) * width] = total
-
-    def rows_of(there):
-        return pl.ds(pl.multiple_of(there * rows, rows), rows)
-
-    def a_copy(other):
-        there = lax.rem(me_y + other, count_y)
-        return pltpu.make_async_remote_copy(
-            src_ref=part_a.at[rows_of(there)], dst_ref=got_a.at[other],
-            send_sem=a_send.at[other], recv_sem=a_recv.at[other],
-            device_id={"gx": me_x, "gy": there}, device_id_type=MESH,
-        )
-
-    def b_copy(other):
-        there = lax.rem(me_y + other, count_y)
-        return pltpu.make_async_remote_copy(
-            src_ref=part_b.at[rows_of(there)], dst_ref=got_b.at[other],
-            send_sem=b_send.at[other], recv_sem=b_recv.at[other],
-            device_id={"gx": me_x + 1, "gy": there}, device_id_type=MESH,
+    back_mid = placed(c_mid.T, g_self)
+    back = jnp.concatenate(
+        [backs[g] + jnp.where(g_mid == g, back_mid, 0.0) for g in range(GROUPS)], axis=0
+    )
+    half = rows // 2
+    for there in range(count_y):
+        start = there * rows
+        part_b[there] = jnp.concatenate(
+            [back[start : start + half], back[start + half : start + rows]], axis=1
         )
 
     @pl.when(exists(1, 0))
@@ -405,12 +412,14 @@
         for other in range(count_y):
             b_copy(other).start()
 
+    strip = jnp.concatenate([level, ahead + placed(c_mid, g_mid)], axis=1)
+    for g in range(GROUPS):
+        part_a[g * width : (g + 1) * width] = (
+            jnp.where(g_self == g, strip, 0.0) + jnp.where(g_side == g, back_side, 0.0)
+        )
+
     for other in range(1, count_y):
         a_copy(other).start()
-
-    @pl.when(jnp.logical_not(exists(-1, 0)))
-    def _():
-        got_b[...] = jnp.zeros(got_b.shape, jnp.float32)
 
     total = part_a[rows_of(me_y), :]
     for other in range(1, count_y):
@@ -426,7 +435,8 @@
     total = got_b[0]
     for other in range(1, count_y):
         total = total + got_b[other]
-    out[0, :, : GROUPS * width] = total[:, : GROUPS * width]
+    out[0, :half, : GROUPS * width] = total[:, : GROUPS * width]
+    out[0, half:, : GROUPS * width] = total[:, GROUPS * width :]
 
     for slot, (step_x, step_y) in enumerate(RING):
         @pl.when(exists(-step_x, -step_y))
@@ -475,9 +485,9 @@
             pltpu.VMEM((width, comps, span_x, span_z), f32),
             pltpu.VMEM((2, comps * width, span_z), f32),
             pltpu.VMEM((GROUPS * width, lanes), f32),
-            pltpu.VMEM((GROUPS * width, lanes), f32),
+            pltpu.VMEM((counts[1], rows // 2, lanes), f32),
             pltpu.VMEM((counts[1], rows, lanes), f32),
-            pltpu.VMEM((counts[1], rows, lanes), f32),
+            pltpu.VMEM((counts[1], rows // 2, lanes), f32),
             dma((4,)),
             dma((len(RING),)), dma((len(RING),)),
             dma((len(HELD),)), dma((len(HELD),)),

time: 15.9 us -> 15.8 us (level)
  no operation moved by 1% of the time
where the time goes in v4:
time: 15.8 us; the launch traced here: 15.7 us
  Pallas kernels  15.1 us (96%)
  local copies, waits for them, and re-layouts  0.61 us (4%)
    pallas_call x1, Pallas kernels, shards(): pl.pallas_call(functools.partial(kernel, (width, span_x, span_y, span_z),...  15.1 us
    unnamed x1, local copies, waits for them, and re-layouts  0.61 us

profile of v4, /device:TPU:0, one launch (start us, length us, event | category | flops | bytes accessed | tf_op | source)
XLA Modules:
  0.0 15.7 jit_solution(10089126158156856107)
XLA Ops:
  0.0 15.1 %shard_map.46 = f32[1,16,192]{2,1,0:T(8,128)S(1)} custom-call(f32[16,3,4,8,128]{4,3,2,1,0:T(8,128)} %modes.1, s32[4,8,128]{2,1,0:T(8,128)} %region.1, f32[16]{0:T(128)} %stiff_in.1, s32[4,8]{1,0:T(4,128)} %bitcast.1), custom_call_target="tpu_custom_call" | custom-call | tf_op jit(solution)/shard_map/pallas_call | solution.py:464
  15.1 0.6 %copy.6 = f32[1,16,192]{2,1,0:T(8,128)} copy(f32[1,16,192]{2,1,0:T(8,128)S(1)} %shard_map.46) | data formatting | bytes 24576

commit v5 on v4

--- a/solution.py
+++ b/solution.py
@@ -140,10 +140,10 @@
         edge_x = 0 if step_x > 0 else span_x - 1
         edge_y = 0 if step_y > 0 else span_y - 1
         if step_x == 0:
-            return region.at[:, edge_y], ring_side.at[(step_y + 1) // 2]
+            return cells.at[:, edge_y], ring_side.at[(step_y + 1) // 2]
         if step_y == 0:
-            return region.at[edge_x], ring_row.at[(step_x + 1) // 2]
-        return region.at[edge_x, edge_y], ring_corner.at[(step_x + 1) + (step_y + 1) // 2]
+            return cells.at[edge_x], ring_row.at[(step_x + 1) // 2]
+        return cells.at[edge_x, edge_y], ring_corner.at[(step_x + 1) + (step_y + 1) // 2]
 
     def ring_copy(slot):
         step_x, step_y = RING[slot]
@@ -157,22 +157,24 @@
     def halo_copy(slot):
         step_x, step_y = HELD[slot]
         if slot < 2:
-            merged = modes.reshape(3 * width, span_x, span_y, span_z)
+            merged = field.reshape(3 * width, span_x, span_y, span_z)
             source, target = merged.at[:, 0, 0 if step_y > 0 else span_y - 1], halo_c.at[slot]
         elif slot == 2:
-            source, target = modes.at[:, :, :, 0], halo_y
+            source, target = field.at[:, :, :, 0], halo_y
         else:
-            source, target = modes.at[:, slot - 3, 0], halo_x.at[slot - 3]
+            source, target = field.at[:, slot - 3, 0], halo_x.at[slot - 3]
         return pltpu.make_async_remote_copy(
             src_ref=source, dst_ref=target,
             send_sem=halo_send.at[slot], recv_sem=halo_recv.at[slot],
             device_id=where_is(-step_x, -step_y), device_id_type=MESH,
         )
 
+    load_region.wait()
     for slot, (step_x, step_y) in enumerate(RING):
         @pl.when(exists(-step_x, -step_y))
         def _():
             ring_copy(slot).start()
+    load_modes.wait()
     for slot, (step_x, step_y) in enumerate(HELD):
         @pl.when(exists(-step_x, -step_y))
         def _():
@@ -197,10 +199,8 @@
 
     load_stiff.wait()
     load_group.wait()
-    load_region.wait()
     for x in range(span_x):
         sigma[1 + x, 1 : 1 + span_y] = stiff_of(cells[x])
-    load_modes.wait()
     flat = field.reshape(3 * width * span_x * span_y, span_z)
     columns = 3 * span_x * span_y
 

time: 15.8 us -> 15.6 us (0.987)
  Pallas kernels: 15.1 us -> 14.8 us
    pallas_call x1, Pallas kernels: 15.1 us -> 14.8 us  [shards(): pl.pallas_call(functools.partial(kernel, (width, span_x, span_y, span_z),...]
where the time goes in v5:
time: 15.6 us; the launch traced here: 15.5 us
  Pallas kernels  14.8 us (95%)
  local copies, waits for them, and re-layouts  0.61 us (4%)
    pallas_call x1, Pallas kernels, shards(): pl.pallas_call(functools.partial(kernel, (width, span_x, span_y, span_z),...  14.8 us
    unnamed x1, local copies, waits for them, and re-layouts  0.61 us

profile of v5, /device:TPU:0, one launch (start us, length us, event | category | flops | bytes accessed | tf_op | source)
XLA Modules:
  0.0 15.5 jit_solution(10781247450537959934)
XLA Ops:
  0.0 14.8 %shard_map.46 = f32[1,16,192]{2,1,0:T(8,128)S(1)} custom-call(f32[16,3,4,8,128]{4,3,2,1,0:T(8,128)} %modes.1, s32[4,8,128]{2,1,0:T(8,128)} %region.1, f32[16]{0:T(128)} %stiff_in.1, s32[4,8]{1,0:T(4,128)} %bitcast.1), custom_call_target="tpu_custom_call" | custom-call | tf_op jit(solution)/shard_map/pallas_call | solution.py:464
  14.9 0.6 %copy.6 = f32[1,16,192]{2,1,0:T(8,128)} copy(f32[1,16,192]{2,1,0:T(8,128)S(1)} %shard_map.46) | data formatting | bytes 24576
